TPU v7x, 256 devices: a whole 4x4x8 slice. The times are simulated.
256 devices in a mesh: vocab: 32 (over z_lo, x, core), seq: 8 (over y, z_hi).
Axes of the slice: x: 4, y: 4, z: 8 (z_hi: 2, z_lo: 4; z = z_hi * 4 + z_lo), core: 2. Of those that a mesh axis runs over, the one named last changes fastest.
Arguments:
- hidden_states: bfloat16 [2048, 3584], P('seq', 'vocab'), may hold values from -6 to 6
- norm_gain: float32 [3584], replicated, may hold values from 0.5 to 1.5
- embedding: bfloat16 [256000, 3584], P(('vocab', 'seq')), may hold values from -0.29882812 to 0.29882812
- targets: int32 [2048], replicated, may hold values from 0 to 255999
Outputs:
- token_loss: float32 [2048], P('seq')
- mean_loss: float32 [], replicated
All inputs are finite; a program needn't handle non-finite values.
Results may differ from a plain program's by a relative error of at most 0.0005.
Values may be sent and summed in bfloat16 or wider, within the bound.
No kernel may reach another device: no remote copies, remote signals or barrier semaphores. Data moves between devices by JAX's collectives and lax.ppermute only.
A program may use at most 64 MiB of HBM per device.

v0:
```python
import jax
import jax.numpy as jnp
from jax import lax
from jax.sharding import Mesh
from jax.sharding import PartitionSpec as P

SEQ = ("seq_0", "seq_1")
VOCAB_SEQ = ("vocab", "seq_0", "seq_1")


def gathered_by_axis(x, axes, dim):
    if not axes:
        return x
    nearer = lax.all_gather(x, axes[-1], axis=dim, tiled=True)
    return gathered_by_axis(nearer, axes[:-1], dim)


def split_up(x, dim, length):
    dims = x.shape
    pieces = x.reshape(*dims[:dim], length, dims[dim] // length, *dims[dim + 1 :])
    return jnp.moveaxis(pieces, dim, 0)


def summed_on_arrival(x, axis, dim):
    pieces = split_up(x, dim, lax.axis_size(axis))
    arrived = lax.all_to_all(pieces, axis, split_axis=0, concat_axis=0, tiled=True)
    return arrived.sum(axis=0)


def copy_for_each(x, axis):
    copies = jnp.broadcast_to(x, (lax.axis_size(axis), *x.shape))
    return lax.all_to_all(copies, axis, split_axis=0, concat_axis=0, tiled=True)


def over_copies(x, axis):
    return copy_for_each(x, axis).sum(axis=0)


def in_one(arrays, axis):
    vector, at, outs = (jnp.concatenate([a.reshape(-1) for a in arrays]), 0, [])
    running = over_copies(vector, axis)
    for a in arrays:
        outs.append(running[at : at + a.size].reshape(a.shape))
        at += a.size
    return tuple(outs)


def normalize(rows, norm_gain):
    values = rows.astype(jnp.float32)
    meansq = jnp.mean(values * values, axis=-1, keepdims=True)
    return (values * lax.rsqrt(meansq + 1e-06) * norm_gain).astype(jnp.bfloat16)


def vocab_terms_of(embedding, targets, normed_rows):
    local_rows = embedding.shape[0]
    base = (lax.axis_index("vocab") * lax.axis_size(SEQ) + lax.axis_index(SEQ)) * local_rows
    scores = jnp.einsum("vd,td->vt", embedding, normed_rows, preferred_element_type=jnp.float32)
    capped = 30.0 * jnp.tanh(scores / 30.0)
    total = jnp.sum(jnp.exp(capped), axis=0)
    ids = base + jnp.arange(local_rows, dtype=jnp.int32)
    hit = ids[:, None] == targets[None, :]
    picked = jnp.sum(jnp.where(hit, capped, 0.0), axis=0)
    return (total, picked)


def local(hidden_states, norm_gain, embedding, targets):
    all_count = targets.shape[0]
    gathered_rows = gathered_by_axis(hidden_states, SEQ, 0)
    whole = lax.all_gather(gathered_rows, "vocab", axis=1, tiled=True)
    normed = normalize(whole, norm_gain)
    total, picked = vocab_terms_of(embedding, targets, normed)
    total, picked = (summed_on_arrival(total, SEQ, 0), summed_on_arrival(picked, SEQ, 0))
    total, picked = in_one((total, picked), "vocab")
    token_loss = jnp.log(total) - picked
    mean_loss = over_copies(jnp.sum(token_loss), SEQ) / all_count
    return (token_loss, mean_loss)


def solution(mesh):
    torus = Mesh(mesh.devices.reshape(mesh.shape["vocab"], 4, 2), ("vocab", "seq_0", "seq_1"))
    placed = (P(SEQ, "vocab"), P(), P(VOCAB_SEQ, None), P())
    return jax.shard_map(
        local, mesh=torus, in_specs=placed, out_specs=(P(SEQ), P()), check_vma=False
    )
```

profile of v0, /device:TPU:1, one launch (start us, length us, event | category | flops | bytes accessed | tf_op | source)
XLA Modules:
  0.0 223.2 jit_solution(5389422925406586718)
XLA Ops:
  7.2 0.0 copy-start.1
  7.2 0.0 copy-start
  7.2 0.0 all-gather.2.cloned.1.call-start
  7.2 10.2 %all_gather.9 = bf16[512,112]{0,1:T(8,128)(2,1)S(1)} all-gather(bf16[256,112]{0,1:T(8,128)(2,1)} %param.4), channel_id=1, replica_groups=mesh['vocab'=32,'seq_0'=4,'seq_1'=2] {'seq_1'}, dimensions={0}, use_global_device_ids=true | all-gather | bytes 172032 | tf_op jit(solution)/shard_map/all_gather | solution.py:14
  17.5 12.0 %all_gather.10 = bf16[2048,112]{0,1:T(8,128)(2,1)} all-gather(bf16[512,112]{0,1:T(8,128)(2,1)S(1)} %all_gather.9), channel_id=1, replica_groups=mesh['vocab'=32,'seq_0'=4,'seq_1'=2] {'seq_0'}, dimensions={0}, use_global_device_ids=true | all-gather | bytes 573440 | tf_op jit(solution)/shard_map/all_gather | solution.py:14
  29.5 0.0 all-gather.2.cloned.1.call-update
  29.5 94.2 %all-gather.2.cloned.1.call-done = bf16[2048,3584]{0,1:T(8,128)(2,1)} async-done(((bf16[2048,112]{0,1:T(8,128)(2,1)}), bf16[2048,3584]{0,1:T(8,128)(2,1)}) %all-gather.2.cloned.1.call-update) | async-done | bytes 14680080 | tf_op jit(solution)/shard_map/all_gather | solution.py:69
  123.7 8.1 %fusion = f32[2048]{0:T(1024)S(1)} fusion(bf16[2048,3584]{0,1:T(8,128)(2,1)} %all-gather.2.cloned.1.call-done), kind=kLoop, calls=%fused_computation.2 | loop fusion | flops 22018048 | bytes 14688256 | tf_op jit(solution)/shard_map/reduce_sum | solution.py:50
  131.8 0.0 copy-done.1
  131.8 0.0 copy-done
  131.8 24.3 %fusion.7 = (f32[2048]{0:T(1024)}, f32[2048]{0:T(1024)S(1)}) fusion(s32[2048]{0:T(1024)S(1)} %copy-done.1, s32[1000]{0:T(1024)S(1)} %iota_add_fusion, bf16[1000,3584]{1,0:T(8,128)(2,1)} %param.6, bf16[2048,3584]{0,1:T(8,128)(2,1)} %all-gather.2.cloned.1.call-done, f32[3584]{0:T(1024)S(1)} %copy-done, f32[2048]{0:T(1024)S(1)} %add_rsqrt_fusion), kind=kOutput, calls=%fused_computation.10 | convolution fusion | flops 14721708032 | bytes 21899168 | tf_op jit(solution)/shard_map/vd,td->vt/dot_general | solution.py:57
  156.0 17.8 %all_to_all.30 = f32[8,1,256]{2,1,0:T(1,128)S(1)} all-to-all(f32[8,1,256]{2,1,0:T(1,128)S(1)} %bitcast.10), channel_id=1, replica_groups=mesh['vocab'=32,'seq_0'=4,'seq_1'=2] {'seq_0','seq_1'}, dimensions={0} | all-to-all | bytes 16384 | tf_op jit(solution)/shard_map/all_to_all | solution.py:26
  173.8 3.3 %all-to-all-start = ((f32[8,1,256]{2,1,0:T(1,128)}), f32[8,1,256]{2,1,0:T(1,128)S(1)}, u32[]{:S(2)}, u32[]{:S(2)}) async-start(f32[8,1,256]{2,1,0:T(1,128)} %bitcast.1), calls=%async_computation | async-start | bytes 16384 | tf_op jit(solution)/shard_map/all_to_all | solution.py:26
  177.1 8.8 %all-to-all-done = f32[8,1,256]{2,1,0:T(1,128)S(1)} async-done(((f32[8,1,256]{2,1,0:T(1,128)}), f32[8,1,256]{2,1,0:T(1,128)S(1)}, u32[]{:S(2)}, u32[]{:S(2)}) %all-to-all-start) | async-done | bytes 8224 | tf_op jit(solution)/shard_map/all_to_all | solution.py:26
  186.1 14.7 %all_to_all.31 = f32[32,1,512]{2,1,0:T(1,128)S(1)} all-to-all(f32[32,1,512]{2,1,0:T(1,128)S(1)} %broadcast_in_dim.15), channel_id=1, replica_groups=mesh['vocab'=32,'seq_0'=4,'seq_1'=2] {'vocab'}, dimensions={0} | all-to-all | bytes 131072 | tf_op jit(solution)/shard_map/all_to_all | solution.py:32
  200.8 0.1 reduce_sum.77
  200.8 1.2 fusion.9
  202.0 0.6 broadcast_in_dim.16
  202.7 11.3 %all_to_all.32 = f32[8,1,1]{2,1,0:T(1,128)S(1)} all-to-all(f32[8,1,1]{2,1,0:T(1,128)S(1)} %broadcast_in_dim.16), channel_id=1, replica_groups=mesh['vocab'=32,'seq_0'=4,'seq_1'=2] {'seq_0','seq_1'}, dimensions={0} | all-to-all | bytes 64 | tf_op jit(solution)/shard_map/all_to_all | solution.py:32
  214.0 0.6 reduce_sum.79
  (6 shorter events, 0.1 us)
Async XLA Ops:
  7.2 124.6 %copy-start.1 = (s32[2048]{0:T(1024)S(1)}, s32[2048]{0:T(1024)}, u32[]{:S(2)}) copy-start(s32[2048]{0:T(1024)} %param.7) | copy-start | bytes 24580
  7.2 124.6 %copy-start = (f32[3584]{0:T(1024)S(1)}, f32[3584]{0:T(1024)}, u32[]{:S(2)}) copy-start(f32[3584]{0:T(1024)} %param.5) | copy-start | bytes 43012
  7.2 116.5 %all-gather.2.cloned.1.call-start = ((), (), s32[]{:S(2)}) async-start(), calls=%async_computation.4 | async-start | bytes 15138816 | tf_op jit(solution)/shard_map/all_gather | solution.py:69
  173.8 12.2 %all-to-all-start = ((f32[8,1,256]{2,1,0:T(1,128)}), f32[8,1,256]{2,1,0:T(1,128)S(1)}, u32[]{:S(2)}, u32[]{:S(2)}) async-start(f32[8,1,256]{2,1,0:T(1,128)} %bitcast.1), calls=%async_computation | async-start | bytes 16384 | tf_op jit(solution)/shard_map/all_to_all | solution.py:26
Sparse Core Ops, SparseCore 0:
  29.6 94.0 all-gather.1
where the time goes:
time: 224 us; the launch traced here: 223 us
  waiting for transfers between devices  103 us (46%)
  blocking collectives  66 us (29%)
  matrix products  24.3 us (11%)
  between operations  15.9 us (7%)
  other arithmetic  10 us (4%)
  starting transfers between devices  3.36 us (2%)
    all_gather x1, waiting for transfers between devices, local(): whole = lax.all_gather(gathered_rows, 'vocab', axis=1, tiled=True)  94.2 us
    all_to_all x2, blocking collectives, copy_for_each(): return lax.all_to_all(copies, axis, split_axis=0, concat_axis=0, tiled=True)  26 us
    dot_general x1, matrix products, vocab_terms_of(): jnp.einsum('vd,td->vt', embedding, normed_rows, preferred_element_type=jn...  24.3 us
    all_gather x2, blocking collectives, gathered_by_axis(): nearer = lax.all_gather(x, axes[-1], axis=dim, tiled=True)  22.2 us
    all_to_all x1, blocking collectives, summed_on_arrival(): lax.all_to_all(pieces, axis, split_axis=0, concat_axis=0, tiled=True)  17.8 us
    all_to_all x1, waiting for transfers between devices, summed_on_arrival(): lax.all_to_all(pieces, axis, split_axis=0, concat_axis=0, tiled=True)  8.85 us
    reduce_sum x1, other arithmetic, normalize(): meansq = jnp.mean(values * values, axis=-1, keepdims=True)  8.09 us
  transfers between devices with their start and end apart: 2, of which 2 were waited for; matrix products, arithmetic and copies ran while one was open for 0% of the time, Pallas kernels for 0%

commit v1 on v0

--- a/solution.py
+++ b/solution.py
@@ -66,7 +66,9 @@
 def local(hidden_states, norm_gain, embedding, targets):
     all_count = targets.shape[0]
     gathered_rows = gathered_by_axis(hidden_states, SEQ, 0)
-    whole = lax.all_gather(gathered_rows, "vocab", axis=1, tiled=True)
+    whole = jnp.concatenate(
+        lax.all_to_all(jnp.stack([gathered_rows] * lax.axis_size("vocab")), "vocab", 0, 0), axis=1
+    )
     normed = normalize(whole, norm_gain)
     total, picked = vocab_terms_of(embedding, targets, normed)
     total, picked = (summed_on_arrival(total, SEQ, 0), summed_on_arrival(picked, SEQ, 0))

time: 224 us -> 465 us (2.08)
  waiting for transfers between devices: 103 us -> 335 us
  between operations: 15.9 us -> 2.49 us
  starting transfers between devices: 3.36 us -> 15 us
  other arithmetic: 10 us -> 17.1 us
  local copies, waits for them, and re-layouts: 0.69 us -> 7.78 us
    all_to_all x0 -> x1, waiting for transfers between devices: none -> 326 us  [local(): lax.all_to_all(jnp.stack([gathered_rows] * lax.axis_size('vocab')), 'voca...]
    all_gather x1 -> x0, waiting for transfers between devices: 94.2 us -> none  [local(): whole = lax.all_gather(gathered_rows, 'vocab', axis=1, tiled=True)]
    all_to_all x0 -> x1, starting transfers between devices: none -> 11.6 us  [local(): lax.all_to_all(jnp.stack([gathered_rows] * lax.axis_size('vocab')), 'voca...]
    another operation x0 -> x1, local copies, waits for them, and re-layouts: none -> 7.08 us  [local(): jnp.stack([gathered_rows] * lax.axis_size('vocab'))]
    convert_element_type x0 -> x1, other arithmetic: none -> 7.05 us  [normalize(): return (values * lax.rsqrt(meansq + 1e-06) * norm_gain).astype(jnp.bfloat16)]
where the time goes in v1:
time: 465 us
  waiting for transfers between devices  335 us (72%)
  blocking collectives  66.7 us (14%)
  matrix products  21.1 us (5%)
  other arithmetic  17.1 us (4%)
  starting transfers between devices  15 us (3%)
  local copies, waits for them, and re-layouts  7.78 us (2%)
    all_to_all x1, waiting for transfers between devices, local(): lax.all_to_all(jnp.stack([gathered_rows] * lax.axis_size('vocab')), 'voca...  326 us
    all_to_all x2, blocking collectives, copy_for_each(): return lax.all_to_all(copies, axis, split_axis=0, concat_axis=0, tiled=True)  25.3 us
    dot_general x1, matrix products, vocab_terms_of(): jnp.einsum('vd,td->vt', embedding, normed_rows, preferred_element_type=jn...  21.1 us
    all_gather x2, blocking collectives, gathered_by_axis(): nearer = lax.all_gather(x, axes[-1], axis=dim, tiled=True)  21 us
    all_to_all x1, blocking collectives, summed_on_arrival(): lax.all_to_all(pieces, axis, split_axis=0, concat_axis=0, tiled=True)  20.4 us
    all_to_all x1, starting transfers between devices, local(): lax.all_to_all(jnp.stack([gathered_rows] * lax.axis_size('vocab')), 'voca...  11.6 us
  transfers between devices with their start and end apart: 2, of which 2 were waited for; matrix products, arithmetic and copies ran while one was open for 0% of the time, Pallas kernels for 0%

profile of v1, /device:TPU:1, one launch (start us, length us, event | category | flops | bytes accessed | tf_op | source)
XLA Modules:
  0.0 464.7 jit_solution(12748186865320753039)
XLA Ops:
  0.6 10.2 %all_gather.6 = bf16[512,112]{0,1:T(8,128)(2,1)S(1)} all-gather(bf16[256,112]{0,1:T(8,128)(2,1)} %param.4), channel_id=1, replica_groups=mesh['vocab'=32,'seq_0'=4,'seq_1'=2] {'seq_1'}, dimensions={0}, use_global_device_ids=true | all-gather | bytes 172032 | tf_op jit(solution)/shard_map/all_gather | solution.py:14
  10.9 10.8 %all_gather.7 = bf16[2048,112]{0,1:T(8,128)(2,1)S(1)} all-gather(bf16[512,112]{0,1:T(8,128)(2,1)S(1)} %all_gather.6), channel_id=1, replica_groups=mesh['vocab'=32,'seq_0'=4,'seq_1'=2] {'seq_0'}, dimensions={0}, use_global_device_ids=true | all-gather | bytes 573440 | tf_op jit(solution)/shard_map/all_gather | solution.py:14
  21.6 7.1 %stack.2 = bf16[32,2048,112]{1,2,0:T(8,128)(2,1)} broadcast(bf16[2048,112]{0,1:T(8,128)(2,1)S(1)} %all_gather.7), dimensions={1,2} | broadcast | bytes 15138816 | tf_op jit(solution)/shard_map/stack | solution.py:70
  28.7 11.6 %all-to-all-start = ((bf16[32,2048,112]{1,2,0:T(8,128)(2,1)}), bf16[32,2048,112]{1,2,0:T(8,128)(2,1)}, u32[]{:S(2)}, u32[]{:S(2)}) async-start(bf16[32,2048,112]{1,2,0:T(8,128)(2,1)} %stack.2), calls=%async_computation | async-start | bytes 29360128 | tf_op jit(solution)/shard_map/all_to_all | solution.py:70
  40.4 0.0 copy-start
  40.4 325.7 %all-to-all-done = bf16[32,2048,112]{1,2,0:T(8,128)(2,1)} async-done(((bf16[32,2048,112]{1,2,0:T(8,128)(2,1)}), bf16[32,2048,112]{1,2,0:T(8,128)(2,1)}, u32[]{:S(2)}, u32[]{:S(2)}) %all-to-all-start) | async-done | bytes 14680096 | tf_op jit(solution)/shard_map/all_to_all | solution.py:70
  366.1 8.1 %multiply_reduce_fusion = f32[2048]{0:T(1024)S(1)} fusion(bf16[32,2048,112]{1,2,0:T(8,128)(2,1)} %all-to-all-done), kind=kLoop, calls=%fused_computation.3 | loop fusion | flops 22018048 | bytes 14688256 | tf_op jit(solution)/shard_map/reduce_sum | solution.py:50
  374.2 0.0 copy-done
  374.2 0.0 copy-start.1
  374.2 7.0 %fusion.1 = bf16[2048,3584]{0,1:T(8,128)(2,1)S(1)} fusion(f32[3584]{0:T(1024)S(1)} %copy-done, f32[2048]{0:T(1024)S(1)} %add_rsqrt_fusion, bf16[32,2048,112]{1,2,0:T(8,128)(2,1)} %all-to-all-done), kind=kLoop, calls=%fused_computation.2 | loop fusion | flops 29360128 | bytes 29382656 | tf_op jit(solution)/shard_map/convert_element_type | solution.py:51
  381.3 0.0 copy-done.1
  381.3 21.1 %fusion.2 = (f32[2048]{0:T(1024)}, f32[2048]{0:T(1024)S(1)}) fusion(s32[2048]{0:T(1024)S(1)} %copy-done.1, s32[1000]{0:T(1024)S(1)} %iota_add_fusion, bf16[2048,3584]{0,1:T(8,128)(2,1)S(1)} %fusion.1, bf16[1000,3584]{1,0:T(8,128)(2,1)} %param.6), kind=kOutput, calls=%fused_computation.6 | convolution fusion | flops 14692347904 | bytes 21876640 | tf_op jit(solution)/shard_map/vd,td->vt/dot_general | solution.py:57
  402.4 20.4 %all_to_all.35 = f32[8,1,256]{2,1,0:T(1,128)S(1)} all-to-all(f32[8,1,256]{2,1,0:T(1,128)S(1)} %bitcast.19), channel_id=1, replica_groups=mesh['vocab'=32,'seq_0'=4,'seq_1'=2] {'seq_0','seq_1'}, dimensions={0} | all-to-all | bytes 16384 | tf_op jit(solution)/shard_map/all_to_all | solution.py:26
  422.8 3.3 all-to-all-start.1
  426.2 8.8 %all-to-all-done.1 = f32[8,1,256]{2,1,0:T(1,128)S(1)} async-done(((f32[8,1,256]{2,1,0:T(1,128)}), f32[8,1,256]{2,1,0:T(1,128)S(1)}, u32[]{:S(2)}, u32[]{:S(2)}) %all-to-all-start.1) | async-done | bytes 8224 | tf_op jit(solution)/shard_map/all_to_all | solution.py:26
  435.1 14.0 %all_to_all.36 = f32[32,1,512]{2,1,0:T(1,128)S(1)} all-to-all(f32[32,1,512]{2,1,0:T(1,128)S(1)} %broadcast_in_dim.15), channel_id=1, replica_groups=mesh['vocab'=32,'seq_0'=4,'seq_1'=2] {'vocab'}, dimensions={0} | all-to-all | bytes 131072 | tf_op jit(solution)/shard_map/all_to_all | solution.py:32
  449.1 0.1 reduce_sum.77
  449.2 1.2 fusion.4
  450.4 0.6 broadcast_in_dim.16
  451.0 11.3 %all_to_all.37 = f32[8,1,1]{2,1,0:T(1,128)S(1)} all-to-all(f32[8,1,1]{2,1,0:T(1,128)S(1)} %broadcast_in_dim.16), channel_id=1, replica_groups=mesh['vocab'=32,'seq_0'=4,'seq_1'=2] {'seq_0','seq_1'}, dimensions={0} | all-to-all | bytes 64 | tf_op jit(solution)/shard_map/all_to_all | solution.py:32
  462.3 0.6 reduce_sum.79
  (6 shorter events, 0.1 us)
Async XLA Ops:
  28.7 337.4 %all-to-all-start = ((bf16[32,2048,112]{1,2,0:T(8,128)(2,1)}), bf16[32,2048,112]{1,2,0:T(8,128)(2,1)}, u32[]{:S(2)}, u32[]{:S(2)}) async-start(bf16[32,2048,112]{1,2,0:T(8,128)(2,1)} %stack.2), calls=%async_computation | async-start | bytes 29360128 | tf_op jit(solution)/shard_map/all_to_all | solution.py:70
  40.4 333.9 %copy-start = (f32[3584]{0:T(1024)S(1)}, f32[3584]{0:T(1024)}, u32[]{:S(2)}) copy-start(f32[3584]{0:T(1024)} %param.5) | copy-start | bytes 43012
  374.2 7.1 %copy-start.1 = (s32[2048]{0:T(1024)S(1)}, s32[2048]{0:T(1024)}, u32[]{:S(2)}) copy-start(s32[2048]{0:T(1024)} %param.7) | copy-start | bytes 24580
  422.8 12.2 %all-to-all-start.1 = ((f32[8,1,256]{2,1,0:T(1,128)}), f32[8,1,256]{2,1,0:T(1,128)S(1)}, u32[]{:S(2)}, u32[]{:S(2)}) async-start(f32[8,1,256]{2,1,0:T(1,128)} %bitcast.3), calls=%async_computation.1 | async-start | bytes 16384 | tf_op jit(solution)/shard_map/all_to_all | solution.py:26
